TPU v7x, 32 devices: a whole 2x2x4 slice. The times are simulated.
32 devices in a mesh: row: 4 (over y, core), col: 8 (over z, x).
Axes of the slice: x: 2, y: 2, z: 4, core: 2. Of those that a mesh axis runs over, the one named last changes fastest.
Arguments:
- matrix: bfloat16 [6144, 6144], P('row', 'col'), as said below
- polar_factor: bfloat16 [6144, 6144], P('row', 'col'), as said below
- start_basis: bfloat16 [6144, 6144], P('row', 'col'), may hold values from -0.078125 to 0.078125
Outputs:
- gram_halves: float32 [3072, 6144], P('row', 'col')
- projected: float32 [3072, 6144], P('row', 'col')
Inputs may be any that keep to these rules, and one draw needn't show every extreme that they name: `matrix`: symmetric. `polar_factor`: symmetric.
All inputs are finite; a program needn't handle non-finite values.
Results may differ from a plain program's by a relative error of at most 0.017.
Values may be sent and summed in bfloat16 or wider, within the bound.
A program may use at most 128 MiB of HBM per device.

v0:
```python
import jax
import jax.numpy as jnp
from jax import lax
from jax.sharding import PartitionSpec as P


def transposed_product(left, right):
    return lax.dot_general(
        left, right, (((0,), (0,)), ((), ())), preferred_element_type=jnp.float32
    )


def per_device(matrix, polar_factor, start_basis):
    local_rows, width = start_basis.shape
    col_count = lax.axis_size("col")
    half_block = width // 2
    half_width = half_block * col_count
    sign = jnp.where(jnp.arange(width) < half_block, 1.0, -1.0).astype(jnp.float32)
    start_cols = lax.all_gather(start_basis, "row", axis=0, tiled=True)
    rows_here = start_cols
    product = jnp.dot(
        lax.all_gather(polar_factor, "col", axis=1, tiled=True),
        rows_here,
        preferred_element_type=jnp.float32,
    )
    basis = ((start_basis.astype(jnp.float32) + sign * product) * 0.5).astype(jnp.bfloat16)
    basis_cols = lax.all_gather(basis, "row", axis=0, tiled=True)
    rows_here = basis_cols
    image = jnp.dot(
        lax.all_gather(matrix, "col", axis=1, tiled=True),
        rows_here,
        preferred_element_type=jnp.float32,
    )
    image = image.astype(jnp.bfloat16)
    basis_rows = lax.all_gather(basis, "col", axis=1, tiled=True)
    split_rows = basis_rows.reshape(local_rows, col_count, 2, half_block)
    left_first = split_rows[:, :, 0, :].reshape(local_rows, half_width)
    left_second = split_rows[:, :, 1, :].reshape(local_rows, half_width)
    right_first = jnp.concatenate([basis[:, :half_block], image[:, :half_block]], axis=1)
    right_second = jnp.concatenate([basis[:, half_block:], image[:, half_block:]], axis=1)
    first_terms = transposed_product(left_first, right_first)
    second_terms = transposed_product(left_second, right_second)
    summed = lax.psum_scatter(
        jnp.concatenate(
            [
                first_terms[:, :half_block],
                second_terms[:, :half_block],
                first_terms[:, half_block:],
                second_terms[:, half_block:],
            ],
            axis=1,
        ).astype(jnp.bfloat16),
        "row",
        scatter_dimension=0,
        tiled=True,
    ).astype(jnp.float32)
    return (summed[:, :width], summed[:, width:])


def solution(mesh):
    return jax.shard_map(
        per_device,
        mesh=mesh,
        in_specs=(P("row", "col"), P("row", "col"), P("row", "col")),
        out_specs=(P("row", "col"), P("row", "col")),
        check_vma=False,
    )
```

profile of v0, /device:TPU:0, one launch (start us, length us, event | category | flops | bytes accessed | tf_op | source)
XLA Modules:
  0.0 1359.9 jit_solution(8603369672791623960)
XLA Ops:
  7.2 0.0 copy-start.1
  7.2 0.0 all-gather.8.cloned.1.call-start
  7.2 0.7 all-gather.8.cloned.1.call-update
  7.9 0.0 all-gather.6.cloned.1.call-start
  8.0 0.7 all-gather.6.cloned.1.call-update
  8.7 0.0 all-gather.14.cloned.1.call-start
  8.7 0.7 all-gather.14.cloned.1.call-update
  9.4 0.0 all-gather.12.cloned.1.call-start
  9.4 0.0 copy-done.1
  9.4 2.4 copy.5
  11.9 64.6 %all-gather.8.cloned.1.call-done = bf16[6144,768]{1,0:T(8,128)(2,1)} async-done(((bf16[1536,768]{1,0:T(8,128)(2,1)}), bf16[6144,768]{1,0:T(8,128)(2,1)}) %all-gather.8.cloned.1.call-update) | async-done | bytes 9437200 | tf_op jit(solution)/shard_map/all_gather | solution.py:19
  76.5 364.0 %all-gather.6.cloned.1.call-done = bf16[1536,6144]{1,0:T(8,128)(2,1)} async-done(((bf16[1536,768]{1,0:T(8,128)(2,1)}), bf16[1536,6144]{1,0:T(8,128)(2,1)}) %all-gather.6.cloned.1.call-update) | async-done | bytes 18874384 | tf_op jit(solution)/shard_map/all_gather | solution.py:22
  440.5 22.0 %multiply_convert_fusion = bf16[1536,768]{0,1:T(8,128)(2,1)} fusion(bf16[1536,768]{0,1:T(8,128)(2,1)} %copy.5, bf16[1536,6144]{1,0:T(8,128)(2,1)} %all-gather.6.cloned.1.call-done, bf16[6144,768]{1,0:T(8,128)(2,1)} %all-gather.8.cloned.1.call-done, f32[768]{0:T(1024)S(1)} %fusion.7), kind=kOutput, calls=%fused_computation.3 | convolution fusion | flops 14501412864 | bytes 33033216 | tf_op jit(solution)/shard_map/dot_general | solution.py:21
  462.5 0.0 copy-start
  462.5 0.0 all-gather.12.cloned.1.call-update
  462.5 0.0 all-gather.10.cloned.1.call-start
  462.6 0.5 all-gather.10.cloned.1.call-update
  463.1 0.2 reduce-scatter.2.cloned.1.call-start
  463.3 0.8 copy-done
  464.2 1.2 fusion.14
  465.3 339.1 %all-gather.14.cloned.1.call-done = bf16[1536,6144]{1,0:T(8,128)(2,1)} async-done(((bf16[1536,768]{1,0:T(8,128)(2,1)}), bf16[1536,6144]{1,0:T(8,128)(2,1)}) %all-gather.14.cloned.1.call-update) | async-done | bytes 18874384 | tf_op jit(solution)/shard_map/all_gather | solution.py:30
  804.4 66.2 %all-gather.12.cloned.1.call-done = bf16[6144,768]{0,1:T(8,128)(2,1)} async-done(((bf16[1536,768]{0,1:T(8,128)(2,1)}), bf16[6144,768]{0,1:T(8,128)(2,1)}) %all-gather.12.cloned.1.call-update) | async-done | bytes 9437200 | tf_op jit(solution)/shard_map/all_gather | solution.py:27
  870.6 20.7 %fusion = bf16[1536,768]{0,1:T(8,128)(2,1)S(1)} fusion(bf16[6144,768]{0,1:T(8,128)(2,1)} %all-gather.12.cloned.1.call-done, bf16[1536,6144]{1,0:T(8,128)(2,1)} %all-gather.14.cloned.1.call-done), kind=kOutput, calls=%fused_computation.5 | convolution fusion | flops 14496694272 | bytes 30670848 | tf_op jit(solution)/shard_map/dot_general | solution.py:29
  891.4 0.2 fusion.15
  891.5 343.5 %all-gather.10.cloned.1.call-done = bf16[1536,6144]{0,1:T(8,128)(2,1)} async-done(((bf16[1536,768]{0,1:T(8,128)(2,1)}), bf16[1536,6144]{0,1:T(8,128)(2,1)}) %all-gather.10.cloned.1.call-update) | async-done | bytes 18874384 | tf_op jit(solution)/shard_map/all_gather | solution.py:35
  1235.0 0.0 copy-start.2
  1235.0 7.6 fusion.10
  1242.6 0.0 copy-done.2
  1242.7 8.4 convolution_convert_fusion
  1251.0 8.4 convolution_convert_fusion.1
  1259.4 0.7 fusion.11
  1260.1 6.6 pad_maximum_fusion
  1266.8 0.0 reduce-scatter.2.cloned.1.call-update
  1266.8 77.9 %reduce-scatter.2.cloned.1.call-done = bf16[768,1536]{0,1:T(8,128)(2,1)} async-done(((bf16[3072,1536]{0,1:T(8,128)(2,1)}), bf16[768,1536]{0,1:T(8,128)(2,1)}) %reduce-scatter.2.cloned.1.call-update) | async-done | bytes 2359312 | tf_op jit(solution)/shard_map/reduce_scatter | solution.py:43
  1344.7 3.4 fusion.13
  1348.1 3.0 copy.6
  1351.1 1.9 copy.7
  (1 shorter events, 0.0 us)
Async XLA Ops:
  7.2 2.3 copy-start.1
  7.2 69.3 %all-gather.8.cloned.1.call-start = ((), (), s32[]{:S(2)}) async-start(), calls=%async_computation.2 | async-start | bytes 11796480 | tf_op jit(solution)/shard_map/all_gather | solution.py:19
  7.9 432.6 %all-gather.6.cloned.1.call-start = ((), (), s32[]{:S(2)}) async-start(), calls=%async_computation.1 | async-start | bytes 21233664 | tf_op jit(solution)/shard_map/all_gather | solution.py:22
  8.7 795.8 %all-gather.14.cloned.1.call-start = ((), (), s32[]{:S(2)}) async-start(), calls=%async_computation.5 | async-start | bytes 21233664 | tf_op jit(solution)/shard_map/all_gather | solution.py:30
  9.4 861.3 %all-gather.12.cloned.1.call-start = ((), (), s32[]{:S(2)}) async-start(), calls=%async_computation.4 | async-start | bytes 11796480 | tf_op jit(solution)/shard_map/all_gather | solution.py:27
  462.5 1.7 copy-start
  462.5 772.5 %all-gather.10.cloned.1.call-start = ((), (), s32[]{:S(2)}) async-start(), calls=%async_computation.3 | async-start | bytes 21233664 | tf_op jit(solution)/shard_map/all_gather | solution.py:35
  463.1 881.6 %reduce-scatter.2.cloned.1.call-start = ((), (), s32[]{:S(2)}) async-start(), calls=%async_computation.6 | async-start | bytes 11796480 | tf_op jit(solution)/shard_map/reduce_scatter | solution.py:43
  1235.0 7.6 copy-start.2
Sparse Core Ops, SparseCore 0:
  9.5 66.9 all-gather.7
  78.1 362.3 all-gather.5
  442.0 362.3 all-gather.13
  806.4 64.1 all-gather.11
  872.6 362.3 all-gather.9
  1266.9 77.7 reduce-scatter.1
where the time goes:
time: 1360 us
  waiting for transfers between devices  1260 us (93%)
  matrix products  59.5 us (4%)
  local copies, waits for them, and re-layouts  21.3 us (2%)
  between operations  14.2 us (1%)
    all_gather x1, waiting for transfers between devices, per_device(): lax.all_gather(polar_factor, 'col', axis=1, tiled=True)  364 us
    all_gather x1, waiting for transfers between devices, per_device(): basis_rows = lax.all_gather(basis, 'col', axis=1, tiled=True)  343 us
    all_gather x1, waiting for transfers between devices, per_device(): lax.all_gather(matrix, 'col', axis=1, tiled=True)  339 us
    reduce_scatter x1, waiting for transfers between devices, per_device(): lax.psum_scatter(jnp.concatenate([first_terms[:, :half_block], second_ter...  77.9 us
    all_gather x1, waiting for transfers between devices, per_device(): basis_cols = lax.all_gather(basis, 'row', axis=0, tiled=True)  66.2 us
    all_gather x1, waiting for transfers between devices, per_device(): start_cols = lax.all_gather(start_basis, 'row', axis=0, tiled=True)  64.6 us
  transfers between devices with their start and end apart: 6, of which 6 were waited for; matrix products, arithmetic and copies ran while one was open for 3% of the time, Pallas kernels for 0%

commit v1 on v0

--- a/solution.py
+++ b/solution.py
@@ -19,7 +19,7 @@
     start_cols = lax.all_gather(start_basis, "row", axis=0, tiled=True)
     rows_here = start_cols
     product = jnp.dot(
-        lax.all_gather(polar_factor, "col", axis=1, tiled=True),
+        jnp.concatenate(lax.all_gather(polar_factor, "col"), axis=1),
         rows_here,
         preferred_element_type=jnp.float32,
     )

time: 1360 us -> 1360 us (level)
  waiting for transfers between devices: 1260 us -> 1230 us
  local copies, waits for them, and re-layouts: 21.3 us -> 45.4 us
    reshape x0 -> x1, local copies, waits for them, and re-layouts: none -> 24.1 us  [per_device(): jnp.concatenate(lax.all_gather(polar_factor, 'col'), axis=1)]
    all_gather x1, waiting for transfers between devices: 64.6 us -> 41.6 us  [per_device(): start_cols = lax.all_gather(start_basis, 'row', axis=0, tiled=True)]
  transfers between devices with their start and end apart: 6 -> 6, of which waited for: 6 -> 6; matrix products, arithmetic and copies ran while one was open for 3% -> 5% of each run, Pallas kernels for 0% -> 0%
where the time goes in v1:
time: 1360 us
  waiting for transfers between devices  1230 us (90%)
  matrix products  59.3 us (4%)
  local copies, waits for them, and re-layouts  45.4 us (3%)
  between operations  14.2 us (1%)
    all_gather x1, waiting for transfers between devices, per_device(): lax.all_gather(polar_factor, 'col')  363 us
    all_gather x1, waiting for transfers between devices, per_device(): basis_rows = lax.all_gather(basis, 'col', axis=1, tiled=True)  343 us
    all_gather x1, waiting for transfers between devices, per_device(): lax.all_gather(matrix, 'col', axis=1, tiled=True)  339 us
    reduce_scatter x1, waiting for transfers between devices, per_device(): lax.psum_scatter(jnp.concatenate([first_terms[:, :half_block], second_ter...  77.9 us
    all_gather x1, waiting for transfers between devices, per_device(): basis_cols = lax.all_gather(basis, 'row', axis=0, tiled=True)  66.2 us
    all_gather x1, waiting for transfers between devices, per_device(): start_cols = lax.all_gather(start_basis, 'row', axis=0, tiled=True)  41.6 us
  transfers between devices with their start and end apart: 6, of which 6 were waited for; matrix products, arithmetic and copies ran while one was open for 5% of the time, Pallas kernels for 0%

profile of v1, /device:TPU:0, one launch (start us, length us, event | category | flops | bytes accessed | tf_op | source)
XLA Modules:
  0.0 1359.9 jit_solution(9861259123497477224)
XLA Ops:
  7.2 0.0 copy-start.1
  7.2 0.0 all-gather.15.cloned.1.call-start
  7.2 0.7 all-gather.15.cloned.1.call-update
  7.9 0.0 all-gather.7.cloned.1.call-start
  8.0 0.7 all-gather.7.cloned.1.call-update
  8.7 0.0 all-gather.13.cloned.1.call-start
  8.7 0.7 all-gather.13.cloned.1.call-update
  9.4 0.0 all-gather.11.cloned.1.call-start
  9.4 0.0 copy-done.1
  9.4 2.4 copy.11
  11.9 362.8 %all-gather.15.cloned.1.call-done = bf16[12288,768]{1,0:T(8,128)(2,1)} async-done(((bf16[1536,768]{1,0:T(8,128)(2,1)}), bf16[12288,768]{1,0:T(8,128)(2,1)}) %all-gather.15.cloned.1.call-update) | async-done | bytes 18874384 | tf_op jit(solution)/shard_map/all_gather | solution.py:22
  374.7 0.0 copy-start.2
  374.7 24.1 %copy.12 = bf16[1536,8,768]{0,2,1:T(8,128)(2,1)} copy(bf16[1536,8,768]{2,0,1:T(8,128)(2,1)} %bitcast.16) | data formatting | bytes 37748736 | tf_op jit(solution)/shard_map/reshape | solution.py:22
  398.8 41.6 %all-gather.7.cloned.1.call-done = bf16[6144,768]{1,0:T(8,128)(2,1)} async-done(((bf16[1536,768]{1,0:T(8,128)(2,1)}), bf16[6144,768]{1,0:T(8,128)(2,1)}) %all-gather.7.cloned.1.call-update) | async-done | bytes 9437200 | tf_op jit(solution)/shard_map/all_gather | solution.py:19
  440.4 0.0 copy-done.2
  440.4 21.8 %multiply_convert_fusion = bf16[1536,768]{0,1:T(8,128)(2,1)} fusion(bf16[1536,768]{0,1:T(8,128)(2,1)S(1)} %copy-done.2, bf16[1536,6144]{0,1:T(8,128)(2,1)} %bitcast.17, bf16[6144,768]{1,0:T(8,128)(2,1)} %all-gather.7.cloned.1.call-done, f32[768]{0:T(1024)S(1)} %fusion.7), kind=kOutput, calls=%fused_computation.3 | convolution fusion | flops 14501412864 | bytes 33033216 | tf_op jit(solution)/shard_map/dot_general | solution.py:21
  462.2 0.0 copy-start
  462.2 0.0 all-gather.11.cloned.1.call-update
  462.3 0.0 all-gather.9.cloned.1.call-start
  462.3 0.5 all-gather.9.cloned.1.call-update
  462.9 0.2 reduce-scatter.2.cloned.1.call-start
  463.1 0.8 copy-done
  463.9 1.2 fusion.14
  465.1 339.3 %all-gather.13.cloned.1.call-done = bf16[1536,6144]{1,0:T(8,128)(2,1)} async-done(((bf16[1536,768]{1,0:T(8,128)(2,1)}), bf16[1536,6144]{1,0:T(8,128)(2,1)}) %all-gather.13.cloned.1.call-update) | async-done | bytes 18874384 | tf_op jit(solution)/shard_map/all_gather | solution.py:30
  804.4 66.2 %all-gather.11.cloned.1.call-done = bf16[6144,768]{0,1:T(8,128)(2,1)} async-done(((bf16[1536,768]{0,1:T(8,128)(2,1)}), bf16[6144,768]{0,1:T(8,128)(2,1)}) %all-gather.11.cloned.1.call-update) | async-done | bytes 9437200 | tf_op jit(solution)/shard_map/all_gather | solution.py:27
  870.6 20.7 %fusion = bf16[1536,768]{0,1:T(8,128)(2,1)S(1)} fusion(bf16[6144,768]{0,1:T(8,128)(2,1)} %all-gather.11.cloned.1.call-done, bf16[1536,6144]{1,0:T(8,128)(2,1)} %all-gather.13.cloned.1.call-done), kind=kOutput, calls=%fused_computation.5 | convolution fusion | flops 14496694272 | bytes 30670848 | tf_op jit(solution)/shard_map/dot_general | solution.py:29
  891.4 0.2 fusion.15
  891.5 343.5 %all-gather.9.cloned.1.call-done = bf16[1536,6144]{0,1:T(8,128)(2,1)} async-done(((bf16[1536,768]{0,1:T(8,128)(2,1)}), bf16[1536,6144]{0,1:T(8,128)(2,1)}) %all-gather.9.cloned.1.call-update) | async-done | bytes 18874384 | tf_op jit(solution)/shard_map/all_gather | solution.py:35
  1235.0 0.0 copy-start.3
  1235.0 7.6 fusion.10
  1242.6 0.0 copy-done.3
  1242.6 8.4 convolution_convert_fusion
  1251.0 8.4 convolution_convert_fusion.1
  1259.4 0.7 fusion.11
  1260.1 6.6 pad_maximum_fusion
  1266.7 0.0 reduce-scatter.2.cloned.1.call-update
  1266.8 77.9 %reduce-scatter.2.cloned.1.call-done = bf16[768,1536]{0,1:T(8,128)(2,1)} async-done(((bf16[3072,1536]{0,1:T(8,128)(2,1)}), bf16[768,1536]{0,1:T(8,128)(2,1)}) %reduce-scatter.2.cloned.1.call-update) | async-done | bytes 2359312 | tf_op jit(solution)/shard_map/reduce_scatter | solution.py:43
  1344.7 3.4 fusion.13
  1348.0 3.0 copy.13
  1351.1 1.9 copy.14
  (1 shorter events, 0.0 us)
Async XLA Ops:
  7.2 2.3 copy-start.1
  7.2 367.5 %all-gather.15.cloned.1.call-start = ((), (), s32[]{:S(2)}) async-start(), calls=%async_computation.6 | async-start | bytes 21233664 | tf_op jit(solution)/shard_map/all_gather | solution.py:22
  7.9 432.5 %all-gather.7.cloned.1.call-start = ((), (), s32[]{:S(2)}) async-start(), calls=%async_computation.1 | async-start | bytes 11796480 | tf_op jit(solution)/shard_map/all_gather | solution.py:19
  8.7 795.8 %all-gather.13.cloned.1.call-start = ((), (), s32[]{:S(2)}) async-start(), calls=%async_computation.4 | async-start | bytes 21233664 | tf_op jit(solution)/shard_map/all_gather | solution.py:30
  9.4 861.2 %all-gather.11.cloned.1.call-start = ((), (), s32[]{:S(2)}) async-start(), calls=%async_computation.3 | async-start | bytes 11796480 | tf_op jit(solution)/shard_map/all_gather | solution.py:27
  374.7 65.8 %copy-start.2 = (bf16[1536,768]{0,1:T(8,128)(2,1)S(1)}, bf16[1536,768]{0,1:T(8,128)(2,1)}, u32[]{:S(2)}) copy-start(bf16[1536,768]{0,1:T(8,128)(2,1)} %copy.11) | copy-start | bytes 7077892
  462.2 1.7 copy-start
  462.3 772.8 %all-gather.9.cloned.1.call-start = ((), (), s32[]{:S(2)}) async-start(), calls=%async_computation.2 | async-start | bytes 21233664 | tf_op jit(solution)/shard_map/all_gather | solution.py:35
  462.9 881.8 %reduce-scatter.2.cloned.1.call-start = ((), (), s32[]{:S(2)}) async-start(), calls=%async_computation.5 | async-start | bytes 11796480 | tf_op jit(solution)/shard_map/reduce_scatter | solution.py:43
  1235.0 7.6 copy-start.3
Sparse Core Ops, SparseCore 0:
  9.5 365.1 all-gather.14
  376.2 64.1 all-gather.6
  442.0 362.3 all-gather.12
  806.4 64.1 all-gather.10
  872.6 362.3 all-gather.8
  1266.9 77.7 reduce-scatter.1
